TPU v7x, 32 devices: a whole 2x2x4 slice. The times are simulated.
32 devices in a mesh: grp: 2 (over y), seq: 16 (over z, x, core).
Axes of the slice: x: 2, y: 2, z: 4, core: 2. Of those that a mesh axis runs over, the one named last changes fastest.
Arguments:
- history: bfloat16 [8192, 1024], P(('grp', 'seq')), parts along dimension 0, may hold values from -6 to 6
- candidates: bfloat16 [512, 1024], P(('grp', 'seq')), parts along dimension 0, may hold values from -6 to 6
- lengths: int32 [8], P('grp'), parts along dimension 0, may hold values from 1 to 2048, 4096 in all
- cand_user: int32 [512], P(('grp', 'seq')), parts along dimension 0, may hold values from 0 to 3
- w_in: bfloat16 [1, 1024, 4096], replicated, may hold values from -0.125 to 0.125
- w_out: bfloat16 [1, 1024, 1024], replicated, may hold values from -0.1875 to 0.1875
Outputs:
- history_out: bfloat16 [8192, 1024], P(('grp', 'seq')), parts along dimension 0
- cand_out: bfloat16 [512, 1024], P(('grp', 'seq')), parts along dimension 0
There are 2 independent parts, one for each index of `grp`. A program takes and returns all parts, laid end to end along the dimension named above; an argument that names none is the same for every part. Nothing has to cross between parts.
Inputs may be any that keep to these rules, and one draw needn't show every extreme that they name: Each user's history length is at least 1; the lengths sum to 4096, and one of them is exactly 2048.
All inputs are finite; a program needn't handle non-finite values.
Results may differ from a plain program's by a relative error of at most 0.0075.
Values may be sent and summed in bfloat16 or wider, within the bound.
A program may use at most 128 MiB of HBM per device.

v0:
```python
import jax
import jax.numpy as jnp
from jax import lax
from jax.sharding import PartitionSpec as P

HEADS = 8
WIN = 8


eps = 1e-06


def passed_along(value, axis, by):
    peers = lax.axis_size(axis)
    pairs = [(i, i + by) for i in range(peers) if 0 <= i + by < peers]
    return lax.ppermute(value, axis, pairs)


def layer_norm(rows):
    centred = rows - jnp.mean(rows, axis=-1, keepdims=True)
    return centred * lax.rsqrt(jnp.mean(centred * centred, axis=-1, keepdims=True) + eps)


def segment_of(positions, ends):
    return jnp.sum((positions[:, None] >= ends[None, :]).astype(jnp.int32), axis=1)


def per_device(history, candidates, lengths, cand_user, w_in, w_out):
    rows = history.shape[0]
    width = history.shape[1]
    heads = HEADS
    head_dim = width // heads
    scale = head_dim ** (-0.5)
    reach = (WIN - 1) * rows
    myself = lax.axis_index("seq")
    ends = jnp.cumsum(lengths)
    q_pos = myself * rows + jnp.arange(rows, dtype=jnp.int32)
    q_seg = segment_of(q_pos, ends)
    k_pos = myself * rows - (WIN - 1) * rows + jnp.arange(WIN * rows, dtype=jnp.int32)
    allowed = (k_pos[None, :] >= 0) & (k_pos[None, :] <= q_pos[:, None])
    allowed = allowed & (q_pos[:, None] - k_pos[None, :] < reach)
    allowed = allowed & (segment_of(k_pos, ends)[None, :] == q_seg[:, None])
    x_rows = history
    c_rows = candidates
    normed = layer_norm(x_rows.astype(jnp.float32)).astype(jnp.bfloat16)
    proj = jax.nn.silu(jnp.dot(normed, w_in[0], preferred_element_type=jnp.float32)).astype(
        jnp.bfloat16
    )
    u_all = proj[:, 0:width]
    v_all = proj[:, width : 2 * width]
    q_all = proj[:, 2 * width : 3 * width]
    k_all = proj[:, 3 * width : 4 * width]
    keyval = jnp.stack((k_all, v_all))
    pieces = []
    for back in range(WIN - 1, 0, -1):
        pieces.append(passed_along(keyval, "seq", back))
    pieces.append(keyval)
    window = jnp.concatenate(pieces, axis=1)
    q_heads = q_all.reshape(rows, heads, head_dim)
    k_heads = window[0].reshape(WIN * rows, heads, head_dim)
    v_heads = window[1].reshape(WIN * rows, heads, head_dim)
    scores = (
        jnp.einsum("qhd,khd->hqk", q_heads, k_heads, preferred_element_type=jnp.float32) * scale
    )
    weight = jnp.where(allowed[None], jax.nn.silu(scores), 0.0).astype(jnp.bfloat16)
    attn = jnp.einsum("hqk,khd->qhd", weight, v_heads, preferred_element_type=jnp.float32).reshape(
        rows, width
    )
    y_rows = (layer_norm(attn) * u_all.astype(jnp.float32)).astype(jnp.bfloat16)
    x_rows = (
        x_rows.astype(jnp.float32) + jnp.dot(y_rows, w_out[0], preferred_element_type=jnp.float32)
    ).astype(jnp.bfloat16)
    cnormed = layer_norm(c_rows.astype(jnp.float32)).astype(jnp.bfloat16)
    u_c = jax.nn.silu(
        jnp.dot(cnormed, w_in[0][:, 0:width], preferred_element_type=jnp.float32)
    ).astype(jnp.bfloat16)
    q_c = jax.nn.silu(
        jnp.dot(cnormed, w_in[0][:, 2 * width : 3 * width], preferred_element_type=jnp.float32)
    ).astype(jnp.bfloat16)
    all_queries = lax.all_gather(q_c, "seq", axis=0, tiled=True)
    all_users = lax.all_gather(cand_user, "seq", axis=0, tiled=True)
    total_cands = all_queries.shape[0]
    owned = all_users[:, None] == q_seg[None, :]
    cq_heads = all_queries.reshape(total_cands, heads, head_dim)
    own_k = k_all.reshape(rows, heads, head_dim)
    own_v = v_all.reshape(rows, heads, head_dim)
    cscores = (
        jnp.einsum("chd,khd->hck", cq_heads, own_k, preferred_element_type=jnp.float32) * scale
    )
    cweight = jnp.where(owned[None], jax.nn.silu(cscores), 0.0).astype(jnp.bfloat16)
    partial_value = jnp.einsum(
        "hck,khd->chd", cweight, own_v, preferred_element_type=jnp.float32
    ).reshape(total_cands, width)
    cattn = lax.psum_scatter(partial_value, "seq", scatter_dimension=0, tiled=True)
    y_c = (layer_norm(cattn) * u_c.astype(jnp.float32)).astype(jnp.bfloat16)
    c_rows = (
        c_rows.astype(jnp.float32) + jnp.dot(y_c, w_out[0], preferred_element_type=jnp.float32)
    ).astype(jnp.bfloat16)
    return (x_rows, c_rows)


def solution(mesh):
    placed = (
        P(("grp", "seq"), None),
        P(("grp", "seq"), None),
        P("grp"),
        P(("grp", "seq")),
        P(),
        P(),
    )
    return jax.shard_map(
        per_device,
        mesh=mesh,
        in_specs=placed,
        out_specs=(P(("grp", "seq"), None), P(("grp", "seq"), None)),
        check_vma=False,
    )
```

profile of v0, /device:TPU:17, one launch (start us, length us, event | category | flops | bytes accessed | tf_op | source)
XLA Modules:
  0.0 305.8 jit_solution(16720493728466638786)
XLA Ops:
  9.9 6.1 %multiply_convert_fusion = bf16[256,4096]{1,0:T(8,128)(2,1)S(1)} fusion(bf16[256,1024]{1,0:T(8,128)(2,1)} %param.6, f32[256]{0:T(256)S(1)} %add_rsqrt_fusion.1, f32[256]{0:T(256)S(1)} %broadcast_multiply_fusion.1, bf16[1,1024,4096]{2,1,0:T(8,128)(2,1)} %param.10), kind=kOutput, calls=%fused_computation.5 | convolution fusion | flops 2153775104 | bytes 11012096 | tf_op jit(solution)/shard_map/dot_general | solution.py:46
  16.0 1.4 copy-done.1
  17.4 1.4 slice_bitcast_fusion.2
  21.2 4.1 %collective-permute-start.1 = (bf16[2,256,1024]{2,1,0:T(8,128)(2,1)}, bf16[2,256,1024]{2,1,0:T(8,128)(2,1)}, u32[]{:S(2)}, u32[]{:S(2)}) collective-permute-start(bf16[2,256,1024]{2,1,0:T(8,128)(2,1)} %pad_maximum_fusion), channel_id=1, source_target_pairs={{0,6},{1,7},{2,8},{3,9},{4,10},{5,11},{6,12},{7,13},{8,14},{9,15},... | collective-permute-start | bytes 3145736 | tf_op jit(solution)/shard_map/ppermute | solution.py:16
  25.3 1.9 collective-permute-start.2
  27.2 1.9 collective-permute-start.3
  29.2 1.9 collective-permute-start.4
  31.4 2.0 multiply_convert_fusion.5
  33.5 173.0 %all_gather.7 = bf16[256,1024]{1,0:T(8,128)(2,1)} all-gather(bf16[16,1024]{1,0:T(8,128)(2,1)S(1)} %multiply_convert_fusion.5), channel_id=1, replica_groups=mesh['grp'=2,'seq'=16] {'seq'}, dimensions={0}, use_global_device_ids=true | all-gather | bytes 557056 | tf_op jit(solution)/shard_map/all_gather | solution.py:80
  206.8 2.1 copy.26
  210.3 9.0 %all-reduce = s32[256]{0:T(256)S(1)} all-reduce(s32[256]{0:T(256)S(1)} %dynamic-update-slice), channel_id=1, replica_groups=mesh['grp'=2,'seq'=16] {'seq'}, use_global_device_ids=true, to_apply=%add | all-reduce | flops 256 | bytes 2048
  219.4 3.4 %fusion.17 = f32[8,128,256]{2,1,0:T(8,128)} fusion(bf16[256,8,128]{0,2,1:T(8,128)(2,1)} %bitcast.69, pred[256,256]{1,0:T(8,128)(4,1)S(1)} %broadcast_compare_fusion, bf16[32,8,8,128]{3,2,1,0:T(8,128)(2,1)} %get-tuple-element.4, bf16[256,1024]{1,0:T(8,128)(2,1)} %all_gather.7), kind=kOutput, calls=%fused_computation.21 | convolution fusion | flops 272105472 | bytes 2686976 | tf_op jit(solution)/shard_map/hck,khd->chd/dot_general | solution.py:91
  222.8 2.5 copy.27
  225.5 2.2 collective-permute-start.5
  227.7 5.2 %collective-permute-start.6 = (bf16[2,256,1024]{2,1,0:T(8,128)(2,1)}, bf16[2,256,1024]{2,1,0:T(8,128)(2,1)S(1)}, u32[]{:S(2)}, u32[]{:S(2)}) collective-permute-start(bf16[2,256,1024]{2,1,0:T(8,128)(2,1)} %pad_maximum_fusion), channel_id=1, source_target_pairs={{0,1},{1,2},{2,3},{3,4},{4,5},{5,6},{6,7},{7,8},{8,9},{9,10},{10,1... | collective-permute-start | bytes 3145736 | tf_op jit(solution)/shard_map/ppermute | solution.py:16
  233.0 1.7 fusion.14
  241.3 9.2 %collective-permute-done.5 = bf16[2,256,1024]{2,1,0:T(8,128)(2,1)S(1)} collective-permute-done((bf16[2,256,1024]{2,1,0:T(8,128)(2,1)}, bf16[2,256,1024]{2,1,0:T(8,128)(2,1)S(1)}, u32[]{:S(2)}, u32[]{:S(2)}) %collective-permute-start.5) | collective-permute-done | bytes 1048608 | tf_op jit(solution)/shard_map/ppermute | solution.py:16
  250.6 14.5 %collective-permute-done.6 = bf16[2,256,1024]{2,1,0:T(8,128)(2,1)S(1)} collective-permute-done((bf16[2,256,1024]{2,1,0:T(8,128)(2,1)}, bf16[2,256,1024]{2,1,0:T(8,128)(2,1)S(1)}, u32[]{:S(2)}, u32[]{:S(2)}) %collective-permute-start.6) | collective-permute-done | bytes 1048608 | tf_op jit(solution)/shard_map/ppermute | solution.py:16
  265.2 3.0 slice_bitcast_fusion
  268.2 3.1 %copy.31 = bf16[256,8,8,128]{3,2,1,0:T(8,128)(2,1)} copy(bf16[256,8,8,128]{3,1,2,0:T(8,128)(2,1)S(1)} %get-tuple-element.2) | data formatting | bytes 8388608
  271.2 6.5 %copy.24 = bf16[1,2048,1024]{1,2,0:T(8,128)(2,1)} copy(bf16[1,2048,1024]{2,1,0:T(8,128)(2,1)} %get-tuple-element.3) | data formatting | bytes 8388608 | tf_op jit(solution)/shard_map/reshape;squeeze | solution.py:61
  277.7 11.6 %fusion.86 = (f32[256]{0:T(256)S(1)}, f32[8,128,256]{2,1,0:T(8,128)S(1)}) fusion(bf16[2048,8,128]{0,2,1:T(8,128)(2,1)} %bitcast.66, pred[256,2048]{1,0:T(8,128)(4,1)} %fusion.14, bf16[2048,8,128]{2,1,0:T(8,128)(2,1)} %bitcast.65, bf16[32,8,8,128]{3,2,1,0:T(8,128)(2,1)} %get-tuple-element.6), kind=kOutput, calls=%fused_computation.99 | convolution fusion | flops 2177105664 | bytes 10486784 | tf_op jit(solution)/shard_map/hqk,khd->qhd/dot_general | solution.py:66
  290.9 3.1 %fusion.18 = bf16[256,1024]{1,0:T(8,128)(2,1)} fusion(bf16[1,1024,1024]{2,1,0:T(8,128)(2,1)S(1)} %copy-done, bf16[256,1024]{1,0:T(8,128)(2,1)} %param.6, f32[256,1024]{1,0:T(8,128)} %copy.25, bf16[256,4096]{1,0:T(8,128)(2,1)} %copy-done.1, f32[256]{0:T(256)S(1)} %add_rsqrt_fusion, f32[256]{0:T(256)S(1)} %broadcast_multiply_fusion), kind=kOutput, calls=%fused_computation.22 | convolution fusion | flops 538968064 | bytes 4720640 | tf_op jit(solution)/shard_map/dot_general | solution.py:71
  296.0 2.9 fusion.26
  (55 shorter events, 17.0 us)
Async XLA Ops:
  7.2 283.7 %copy-start = (bf16[1,1024,1024]{2,1,0:T(8,128)(2,1)S(1)}, bf16[1,1024,1024]{2,1,0:T(8,128)(2,1)}, u32[]{:S(2)}) copy-start(bf16[1,1024,1024]{2,1,0:T(8,128)(2,1)} %param.11) | copy-start | bytes 6291460
  7.2 286.8 %reduce-scatter.2.cloned.1.call-start = ((), (), s32[]{:S(2)}) async-start(), calls=%async_computation.1 | async-start | bytes 1114112 | tf_op jit(solution)/shard_map/reduce_scatter | solution.py:94
  16.0 1.4 copy-start.1
  17.4 13.7 %copy-start.2 = (bf16[16,1024]{1,0:T(8,128)(2,1)S(1)}, bf16[16,1024]{1,0:T(8,128)(2,1)}, u32[]{:S(2)}) copy-start(bf16[16,1024]{1,0:T(8,128)(2,1)} %param.7) | copy-start | bytes 98308
  17.4 189.1 %copy-start.3 = (s32[4]{0:T(128)S(1)}, s32[4]{0:T(128)}, u32[]{:S(2)}) copy-start(s32[4]{0:T(128)} %param.8) | copy-start | bytes 52
  17.4 191.4 %copy-start.5 = (u32[32]{0:T(128)S(1)}, u32[32]{0:T(128)}, u32[]{:S(2)}) copy-start(u32[32]{0:T(128)} %constant.50) | copy-start | bytes 388
  17.4 192.7 %copy-start.4 = (s32[16]{0:T(128)S(1)}, s32[16]{0:T(128)}, u32[]{:S(2)}) copy-start(s32[16]{0:T(128)} %param.9) | copy-start | bytes 196
  19.9 205.7 %collective-permute-start = (bf16[2,256,1024]{2,1,0:T(8,128)(2,1)}, bf16[2,256,1024]{2,1,0:T(8,128)(2,1)}, u32[]{:S(2)}, u32[]{:S(2)}) collective-permute-start(bf16[2,256,1024]{2,1,0:T(8,128)(2,1)} %pad_maximum_fusion), channel_id=1, source_target_pairs={{0,7},{1,8},{2,9},{3,10},{4,11},{5,12},{6,13},{7,14},{8,15},{16,23... | collective-permute-start | bytes 3145736 | tf_op jit(solution)/shard_map/ppermute | solution.py:16
  21.2 206.6 %collective-permute-start.1 = (bf16[2,256,1024]{2,1,0:T(8,128)(2,1)}, bf16[2,256,1024]{2,1,0:T(8,128)(2,1)}, u32[]{:S(2)}, u32[]{:S(2)}) collective-permute-start(bf16[2,256,1024]{2,1,0:T(8,128)(2,1)} %pad_maximum_fusion), channel_id=1, source_target_pairs={{0,6},{1,7},{2,8},{3,9},{4,10},{5,11},{6,12},{7,13},{8,14},{9,15},... | collective-permute-start | bytes 3145736 | tf_op jit(solution)/shard_map/ppermute | solution.py:16
  25.3 212.0 %collective-permute-start.2 = (bf16[2,256,1024]{2,1,0:T(8,128)(2,1)}, bf16[2,256,1024]{2,1,0:T(8,128)(2,1)}, u32[]{:S(2)}, u32[]{:S(2)}) collective-permute-start(bf16[2,256,1024]{2,1,0:T(8,128)(2,1)} %pad_maximum_fusion), channel_id=1, source_target_pairs={{0,5},{1,6},{2,7},{3,8},{4,9},{5,10},{6,11},{7,12},{8,13},{9,14},{... | collective-permute-start | bytes 3145736 | tf_op jit(solution)/shard_map/ppermute | solution.py:16
  27.2 211.4 %collective-permute-start.3 = (bf16[2,256,1024]{2,1,0:T(8,128)(2,1)}, bf16[2,256,1024]{2,1,0:T(8,128)(2,1)}, u32[]{:S(2)}, u32[]{:S(2)}) collective-permute-start(bf16[2,256,1024]{2,1,0:T(8,128)(2,1)} %pad_maximum_fusion), channel_id=1, source_target_pairs={{0,4},{1,5},{2,6},{3,7},{4,8},{5,9},{6,10},{7,11},{8,12},{9,13},{1... | collective-permute-start | bytes 3145736 | tf_op jit(solution)/shard_map/ppermute | solution.py:16
  29.2 210.8 %collective-permute-start.4 = (bf16[2,256,1024]{2,1,0:T(8,128)(2,1)}, bf16[2,256,1024]{2,1,0:T(8,128)(2,1)}, u32[]{:S(2)}, u32[]{:S(2)}) collective-permute-start(bf16[2,256,1024]{2,1,0:T(8,128)(2,1)} %pad_maximum_fusion), channel_id=1, source_target_pairs={{0,3},{1,4},{2,5},{3,6},{4,7},{5,8},{6,9},{7,10},{8,11},{9,12},{10... | collective-permute-start | bytes 3145736 | tf_op jit(solution)/shard_map/ppermute | solution.py:16
  225.5 25.0 %collective-permute-start.5 = (bf16[2,256,1024]{2,1,0:T(8,128)(2,1)}, bf16[2,256,1024]{2,1,0:T(8,128)(2,1)S(1)}, u32[]{:S(2)}, u32[]{:S(2)}) collective-permute-start(bf16[2,256,1024]{2,1,0:T(8,128)(2,1)} %pad_maximum_fusion), channel_id=1, source_target_pairs={{0,2},{1,3},{2,4},{3,5},{4,6},{5,7},{6,8},{7,9},{8,10},{9,11},{10,... | collective-permute-start | bytes 3145736 | tf_op jit(solution)/shard_map/ppermute | solution.py:16
  227.7 37.3 %collective-permute-start.6 = (bf16[2,256,1024]{2,1,0:T(8,128)(2,1)}, bf16[2,256,1024]{2,1,0:T(8,128)(2,1)S(1)}, u32[]{:S(2)}, u32[]{:S(2)}) collective-permute-start(bf16[2,256,1024]{2,1,0:T(8,128)(2,1)} %pad_maximum_fusion), channel_id=1, source_target_pairs={{0,1},{1,2},{2,3},{3,4},{4,5},{5,6},{6,7},{7,8},{8,9},{9,10},{10,1... | collective-permute-start | bytes 3145736 | tf_op jit(solution)/shard_map/ppermute | solution.py:16
Sparse Core Ops, SparseCore 0:
  225.5 60.1 reduce-scatter.1
where the time goes:
time: 312 us; the launch traced here: 306 us
  blocking collectives  182 us (58%)
  matrix products  29.2 us (9%)
  local copies, waits for them, and re-layouts  28.7 us (9%)
  waiting for transfers between devices  23.7 us (8%)
  starting transfers between devices  18.6 us (6%)
  between operations  14.9 us (5%)
  other arithmetic  8.52 us (3%)
    all_gather x1, blocking collectives, per_device(): all_queries = lax.all_gather(q_c, 'seq', axis=0, tiled=True)  173 us
    ppermute x7, waiting for transfers between devices, passed_along(): return lax.ppermute(value, axis, pairs)  23.7 us
    ppermute x7, starting transfers between devices, passed_along(): return lax.ppermute(value, axis, pairs)  18.6 us
    unnamed x25, local copies, waits for them, and re-layouts  16.3 us
    dot_general x1, matrix products, per_device(): jnp.einsum('hqk,khd->qhd', weight, v_heads, preferred_element_type=jnp.fl...  11.6 us
    unnamed x1, blocking collectives  9 us
    another operation x1, local copies, waits for them, and re-layouts, per_device(): v_heads = window[1].reshape(WIN * rows, heads, head_dim)  6.49 us
  transfers between devices with their start and end apart: 8, of which 2 were waited for; matrix products, arithmetic and copies ran while one was open for 16% of the time, Pallas kernels for 0%

commit v1 on v0

v1 whole, which is shorter than its diff:
```python
import functools

import jax
import jax.numpy as jnp
from jax import lax
from jax.experimental import pallas as pl
from jax.experimental.pallas import tpu as pltpu
from jax.sharding import PartitionSpec as P

HEADS = 8
WIN = 8
CHUNKS = 2
ROW = 4

eps = 1e-06
bf16 = jnp.bfloat16
f32 = jnp.float32


def layer_norm(rows):
    centred = rows - jnp.mean(rows, axis=-1, keepdims=True)
    return centred * lax.rsqrt(jnp.mean(centred * centred, axis=-1, keepdims=True) + eps)


def silu_of_twice(half):
    return half + half * jnp.tanh(half)


def dot(a, b):
    return jnp.dot(a, b, preferred_element_type=f32)


def dot_t(a, b):
    return lax.dot_general(a, b, (((1,), (1,)), ((), ())), preferred_element_type=f32)


def kernel(
    n,
    lengths,
    hist,
    cand,
    users,
    w_in_hbm,
    w_out_hbm,
    out_ref,
    cout_ref,
    w_in,
    w_out,
    wnd,
    q_s,
    u_s,
    kv_s,
    own_kv,
    acc,
    cbuf,
    ubuf,
    qc_s,
    part,
    buf1,
    buf2,
    buf3,
    w_sem,
    x_send,
    x_recv,
    cz_send,
    cz_recv,
    uz_send,
    uz_recv,
    cx_send,
    cx_recv,
    rz_send,
    rz_recv,
):
    rows, width = hist.shape
    cr = cand.shape[0]
    head_dim = width // HEADS
    half_scale = 0.5 * head_dim ** (-0.5)
    depth = n // ROW
    s = lax.axis_index("seq")
    z = s // ROW
    r = s % ROW
    p = r // 2
    k = r % 2
    piece = rows // CHUNKS
    sibling = s + 1 - 2 * k
    partner = s + 2 - 4 * p

    w_copies = [
        pltpu.make_async_copy(
            w_in_hbm.at[0, :, pl.ds(c * width, width)], w_in.at[c], w_sem.at[c]
        )
        for c in range(4)
    ]
    w_copies.append(pltpu.make_async_copy(w_out_hbm.at[0], w_out, w_sem.at[4]))
    for c in (2, 3, 1, 0, 4):
        w_copies[c].start()

    barrier = pltpu.get_barrier_semaphore()
    pl.semaphore_signal(barrier, inc=1, device_id={"seq": sibling}, device_id_type=pl.DeviceIdType.MESH)
    pl.semaphore_signal(barrier, inc=1, device_id={"seq": partner}, device_id_type=pl.DeviceIdType.MESH)

    def greet(d, carry):
        pl.semaphore_signal(
            barrier,
            inc=1,
            device_id={"seq": (s + ROW * d) % n},
            device_id_type=pl.DeviceIdType.MESH,
        )
        return carry

    lax.fori_loop(1, depth, greet, 0)
    pl.semaphore_wait(barrier, depth + 1)

    def remote(src, dst, send, recv, to):
        return pltpu.make_async_remote_copy(
            src_ref=src,
            dst_ref=dst,
            send_sem=send,
            recv_sem=recv,
            device_id={"seq": to},
            device_id_type=pl.DeviceIdType.MESH,
        )

    def x_copy(src_slot, dst_slot, h, kind, to):
        part_rows = pl.ds(h * piece, piece)
        src = hist.at[part_rows] if src_slot is None else wnd.at[src_slot, part_rows]
        return remote(src, wnd.at[dst_slot, part_rows], x_send.at[kind, h], x_recv.at[dst_slot, h], to)

    own_slot = 2 * ROW + r
    up = (s + ROW) % n

    me_block = k * 2 + p

    def cz_copy(d, which):
        to = (s + ROW * d) % n
        at = pl.ds(pl.multiple_of(z * cr, cr), cr)
        if which == 0:
            return remote(cand, cbuf.at[me_block, at], cz_send.at[d], cz_recv.at[d], to)
        return remote(users, ubuf.at[me_block, at], uz_send.at[d], uz_recv.at[d], to)

    def cz_start(d, carry):
        cz_copy(d, 0).start()
        cz_copy(d, 1).start()
        return carry

    lax.fori_loop(1, depth, cz_start, 0)

    for h in range(CHUNKS):

        @pl.when(z + 1 < depth)
        def _():
            x_copy(None, ROW + r, h, 0, up).start()

        @pl.when(p == 0)
        def _():
            x_copy(None, own_slot, h, 1, partner).start()

        @pl.when(k == 0)
        def _():
            x_copy(None, own_slot, h, 2, sibling).start()

    ends = []
    total = jnp.int32(0)
    for j in range(lengths.shape[0]):
        total = total + lengths[j]
        ends.append(total)

    def seg(pos):
        out = jnp.zeros(pos.shape, jnp.int32)
        for e in ends:
            out = out + (pos >= e).astype(jnp.int32)
        return out

    q_pos = s * rows + lax.broadcasted_iota(jnp.int32, (rows, 1), 0)
    q_seg = seg(q_pos)

    def project(normed, block):
        return silu_of_twice(dot(normed, w_in[block]) * 0.5).astype(bf16)

    def attend(kv, shard):
        k_pos = shard * rows + lax.broadcasted_iota(jnp.int32, (1, rows), 1)
        ok = (k_pos <= q_pos) & (q_pos - k_pos < (WIN - 1) * rows) & (seg(k_pos) == q_seg)
        for h in range(HEADS):
            cols = slice(h * head_dim, (h + 1) * head_dim)
            half = dot_t(q_s[:, cols], kv[0, :, cols]) * half_scale
            weight = jnp.where(ok, silu_of_twice(half), 0.0).astype(bf16)
            acc[:, cols] += dot(weight, kv[1, :, cols])

    acc[...] = jnp.zeros_like(acc)
    normed = layer_norm(hist[...].astype(f32)).astype(bf16)
    w_copies[2].wait()
    q_s[...] = project(normed, 2)
    w_copies[3].wait()
    own_kv[0] = project(normed, 3)

    mine_at = pl.ds(pl.multiple_of(z * cr, cr), cr)
    cbuf[me_block, mine_at] = cand[...]
    ubuf[me_block, mine_at] = users[...]

    def cz_wait(d, carry):
        cz_copy(d, 0).wait_recv()
        cz_copy(d, 1).wait_recv()
        return carry

    lax.fori_loop(1, depth, cz_wait, 0)
    to_partner = [
        remote(cbuf.at[me_block], cbuf.at[me_block], cx_send.at[0], cx_recv.at[0], partner),
        remote(ubuf.at[me_block], ubuf.at[me_block], cx_send.at[1], cx_recv.at[1], partner),
    ]
    for c in to_partner:
        c.start()
    w_copies[1].wait()
    own_kv[1] = project(normed, 1)
    for c in to_partner:
        c.wait_recv()
    to_sibling = [
        remote(cbuf.at[pl.ds(2 * k, 2)], cbuf.at[pl.ds(2 * k, 2)], cx_send.at[2], cx_recv.at[2], sibling),
        remote(ubuf.at[pl.ds(2 * k, 2)], ubuf.at[pl.ds(2 * k, 2)], cx_send.at[3], cx_recv.at[3], sibling),
    ]
    for c in to_sibling:
        c.start()
    w_copies[0].wait()
    u_s[...] = project(normed, 0)
    attend(own_kv, s)
    for c in to_sibling:
        c.wait_recv()

    def red1():
        return remote(part.at[pl.ds(2 - 2 * k, 2)], buf1, cx_send.at[4], cx_recv.at[4], sibling)

    def red2():
        return remote(part.at[k * 2 + 1 - p], buf2, cx_send.at[5], cx_recv.at[5], partner)

    def red3(d):
        to_row = (z + d) % depth
        src = part.at[me_block, pl.ds(pl.multiple_of(to_row * cr, cr), cr)]
        return remote(src, buf3.at[d], rz_send.at[d], rz_recv.at[d], (s + ROW * d) % n)

    block_rows = depth * cr
    k_row = s * rows + lax.broadcasted_iota(jnp.int32, (1, rows), 1)
    k_seg = seg(k_row)

    def cand_scores(first, count):
        size = count * block_rows
        c_norm = layer_norm(cbuf[pl.ds(first, count)].reshape(size, width).astype(f32)).astype(bf16)
        qc_s[...] = project(c_norm, 2)
        owner = ubuf[pl.ds(first, count)].reshape(size, ubuf.shape[-1])[:, :1]
        ok = owner == k_seg
        for h in range(HEADS):
            cols = slice(h * head_dim, (h + 1) * head_dim)
            half = dot_t(qc_s[:, cols], own_kv[0, :, cols]) * half_scale
            weight = jnp.where(ok, silu_of_twice(half), 0.0).astype(bf16)
            part[pl.ds(first, count), :, cols] = dot(weight, own_kv[1, :, cols]).reshape(
                count, block_rows, head_dim
            )

    count = qc_s.shape[0] // block_rows
    if count == ROW:
        cand_scores(0, ROW)
    else:

        def cand_block(b, carry):
            cand_scores(b * count, count)
            return carry

        lax.fori_loop(0, ROW // count, cand_block, 0)
    red1().start()

    def needed(slot, of):
        return (slot > of) & (slot < 2 * ROW + of) & (z - 2 + slot // ROW >= 0)

    def pair(j, carry):
        base = 2 * ROW - ROW * (j // 2)
        swap = jnp.minimum(j // 2, 1) * p
        first = base + 2 * ((j + swap) % 2)
        mine = first + k

        def hop(h, go_up, go_across):
            pieces = pl.ds(h * piece, piece)
            pltpu.make_async_copy(hist.at[pieces], wnd.at[mine, pieces], x_recv.at[mine, h]).wait()
            if go_up:

                @pl.when((z + 1 < depth) & (r >= 1))
                def _():
                    x_copy(mine, mine - ROW, h, 3, up).start()

            if go_across == 1:
                x_copy(mine, mine, h, 4, partner).start()
            if go_across == 2:

                @pl.when(p == 1)
                def _():
                    x_copy(mine, mine, h, 5, partner).start()

            @pl.when(needed(mine, r + 1 - 2 * k))
            def _():
                x_copy(mine, mine, h, 6 + j, sibling).start()

        @pl.when((j == 0) & (p == 1))
        def _():
            for h in range(CHUNKS):
                hop(h, False, 0)

        @pl.when((j == 2) & (z >= 1))
        def _():
            for h in range(CHUNKS):
                hop(h, True, 1)

        @pl.when((j == 3) & (z >= 1))
        def _():
            for h in range(CHUNKS):
                hop(h, False, 0)

        @pl.when((j == 4) & (z >= 2) & (r >= 1))
        def _():
            for h in range(CHUNKS):
                hop(h, False, 2)

        @pl.when((j == 5) & (z >= 2) & (p == 0))
        def _():
            for h in range(CHUNKS):
                hop(h, False, 0)

        @pl.when(j == 2)
        def _():
            red1().wait_recv()
            part[pl.ds(2 * k, 2)] += buf1[...]
            red2().start()

        @pl.when(j == 3)
        def _():
            red2().wait_recv()
            part[me_block] += buf2[...]

            def send(d, c):
                red3(d).start()
                return c

            lax.fori_loop(1, depth, send, 0)

        def one(m, c):
            slot = first + (k + m) % 2

            @pl.when(needed(slot, r))
            def _():
                @pl.when(m == 1)
                def _():
                    for h in range(CHUNKS):
                        pieces = pl.ds(h * piece, piece)
                        pltpu.make_async_copy(
                            hist.at[pieces], wnd.at[slot, pieces], x_recv.at[slot, h]
                        ).wait()

                norm = layer_norm(wnd[slot].astype(f32)).astype(bf16)
                kv_s[0] = project(norm, 3)
                kv_s[1] = project(norm, 1)
                attend(kv_s, (z - 2) * ROW + slot)

            return c

        return lax.fori_loop(0, 2, one, carry)

    lax.fori_loop(0, 6, pair, 0)

    w_copies[4].wait()
    y = (layer_norm(acc[...]) * u_s[...].astype(f32)).astype(bf16)
    out_ref[...] = (hist[...].astype(f32) + dot(y, w_out[...])).astype(bf16)

    u_c = project(layer_norm(cand[...].astype(f32)).astype(bf16), 0)

    def take(d, c):
        red3(d).wait_recv()
        return c + buf3[d]

    mine_sum = part[me_block, mine_at]
    cattn = lax.fori_loop(1, depth, take, mine_sum)
    y_c = (layer_norm(cattn) * u_c.astype(f32)).astype(bf16)
    cout_ref[...] = (cand[...].astype(f32) + dot(y_c, w_out[...])).astype(bf16)

    for c in to_partner + to_sibling + [red1(), red2()]:
        c.wait_send()

    def left(d, c):
        cz_copy(d, 0).wait_send()
        cz_copy(d, 1).wait_send()
        red3(d).wait_send()
        return c

    lax.fori_loop(1, depth, left, 0)
    for h in range(CHUNKS):

        @pl.when(z + 1 < depth)
        def _():
            x_copy(None, ROW + r, h, 0, up).wait_send()

        @pl.when(p == 0)
        def _():
            x_copy(None, own_slot, h, 1, partner).wait_send()

        @pl.when(k == 0)
        def _():
            x_copy(None, own_slot, h, 2, sibling).wait_send()

        @pl.when((z >= 1) & (z + 1 < depth) & (r >= 1))
        def _():
            x_copy(ROW + r, r, h, 3, up).wait_send()

        @pl.when(z >= 1)
        def _():
            x_copy(ROW + r, ROW + r, h, 4, partner).wait_send()

        @pl.when((z >= 2) & (p == 1))
        def _():
            x_copy(r, r, h, 5, partner).wait_send()

        other = r + 1 - 2 * k
        across = 2 * (1 - p) + k

        @pl.when((p == 1) & needed(2 * ROW + k, other))
        def _():
            x_copy(2 * ROW + k, 2 * ROW + k, h, 6, sibling).wait_send()

        @pl.when((z >= 1) & needed(ROW + r, other))
        def _():
            x_copy(ROW + r, ROW + r, h, 8, sibling).wait_send()

        @pl.when((z >= 1) & needed(ROW + across, other))
        def _():
            x_copy(ROW + across, ROW + across, h, 9, sibling).wait_send()

        @pl.when((z >= 2) & (r >= 1) & needed(r, other))
        def _():
            x_copy(r, r, h, 10, sibling).wait_send()

        @pl.when((z >= 2) & (p == 0) & needed(across, other))
        def _():
            x_copy(across, across, h, 11, sibling).wait_send()


def per_device(n, history, candidates, lengths, cand_user, w_in, w_out):
    rows, width = history.shape
    cr = candidates.shape[0]
    depth = n // ROW
    users = jnp.broadcast_to(cand_user[:, None], (cr, 128))
    vmem = pl.BlockSpec(memory_space=pltpu.VMEM)
    dma = pltpu.SemaphoreType.DMA
    block = depth * cr
    many = ROW * block if ROW * block <= 512 else block
    return pl.pallas_call(
        functools.partial(kernel, n),
        out_shape=(
            jax.ShapeDtypeStruct((rows, width), bf16),
            jax.ShapeDtypeStruct((cr, width), bf16),
        ),
        in_specs=[
            pl.BlockSpec(memory_space=pltpu.SMEM),
            vmem,
            vmem,
            vmem,
            pl.BlockSpec(memory_space=pl.ANY),
            pl.BlockSpec(memory_space=pl.ANY),
        ],
        out_specs=(vmem, vmem),
        scratch_shapes=[
            pltpu.VMEM((4, width, width), bf16),
            pltpu.VMEM((width, width), bf16),
            pltpu.VMEM((3 * ROW, rows, width), bf16),
            pltpu.VMEM((rows, width), bf16),
            pltpu.VMEM((rows, width), bf16),
            pltpu.VMEM((2, rows, width), bf16),
            pltpu.VMEM((2, rows, width), bf16),
            pltpu.VMEM((rows, width), f32),
            pltpu.VMEM((ROW, block, width), bf16),
            pltpu.VMEM((ROW, block, 128), jnp.int32),
            pltpu.VMEM((many, width), bf16),
            pltpu.VMEM((ROW, block, width), f32),
            pltpu.VMEM((2, block, width), f32),
            pltpu.VMEM((block, width), f32),
            pltpu.VMEM((depth, cr, width), f32),
            dma((5,)),
            dma((12, CHUNKS)),
            dma((3 * ROW, CHUNKS)),
            dma((depth,)),
            dma((depth,)),
            dma((depth,)),
            dma((depth,)),
            dma((6,)),
            dma((6,)),
            dma((depth,)),
            dma((depth,)),
        ],
        compiler_params=pltpu.CompilerParams(
            collective_id=0, has_side_effects=True, vmem_limit_bytes=60 * 1024 * 1024
        ),
    )(lengths, history, candidates, users, w_in, w_out)


def solution(mesh):
    n = mesh.shape["seq"]
    placed = (
        P(("grp", "seq"), None),
        P(("grp", "seq"), None),
        P("grp"),
        P(("grp", "seq")),
        P(),
        P(),
    )
    return jax.shard_map(
        functools.partial(per_device, n),
        mesh=mesh,
        in_specs=placed,
        out_specs=(P(("grp", "seq"), None), P(("grp", "seq"), None)),
        check_vma=False,
    )
```

time: 312 us -> 71.6 us (0.23); the launches traced: 306 us -> 71.3 us
  blocking collectives: 182 us -> 0 us
  Pallas kernels: 0 us -> 66.1 us
  matrix products: 29.2 us -> 0 us
  local copies, waits for them, and re-layouts: 28.7 us -> 4.57 us
  waiting for transfers between devices: 23.7 us -> 0 us
  starting transfers between devices: 18.6 us -> 0 us
  between operations: 14.9 us -> 0.64 us
  other arithmetic: 8.52 us -> 0 us
    all_gather x1 -> x0, blocking collectives: 173 us -> none  [per_device(): all_queries = lax.all_gather(q_c, 'seq', axis=0, tiled=True)]
    pallas_call x0 -> x1, Pallas kernels: none -> 66.1 us  [per_device(): pl.pallas_call(functools.partial(kernel, n), out_shape=(jax.ShapeDtypeStr...]
    dot_general x6 -> x0, matrix products: 29.2 us -> none  [the longest x1 11.6 us: per_device(): jnp.einsum('hqk,khd->qhd', weight, v_heads, preferred_element_type=jnp.fl...]
    ppermute x7 -> x0, waiting for transfers between devices: 23.7 us -> none  [passed_along(): return lax.ppermute(value, axis, pairs)]
    ppermute x7 -> x0, starting transfers between devices: 18.6 us -> none  [passed_along(): return lax.ppermute(value, axis, pairs)]
    unnamed x25 -> x2, local copies, waits for them, and re-layouts: 16.3 us -> 3.24 us
    unnamed x1 -> x0, blocking collectives: 9 us -> none
    another operation x1 -> x0, local copies, waits for them, and re-layouts: 6.49 us -> none  [per_device(): v_heads = window[1].reshape(WIN * rows, heads, head_dim)]
  transfers between devices with their start and end apart: 8 -> 0, of which waited for: 2 -> 0; matrix products, arithmetic and copies ran while one was open for 16% -> 0% of each run, Pallas kernels for 0% -> 0%
where the time goes in v1:
time: 71.6 us; the launch traced here: 71.3 us
  Pallas kernels  66.1 us (92%)
  local copies, waits for them, and re-layouts  4.57 us (6%)
    pallas_call x1, Pallas kernels, per_device(): pl.pallas_call(functools.partial(kernel, n), out_shape=(jax.ShapeDtypeStr...  66.1 us
    unnamed x2, local copies, waits for them, and re-layouts  3.24 us

profile of v1, /device:TPU:17, one launch (start us, length us, event | category | flops | bytes accessed | tf_op | source)
XLA Modules:
  0.0 71.3 jit_solution(14981656257247457577)
XLA Ops:
  0.6 1.3 %broadcast_in_dim.2.users = s32[16,128]{1,0:T(8,128)} broadcast(s32[16]{0:T(128)} %param.9), dimensions={0} | broadcast | bytes 8256 | tf_op jit(solution)/shard_map/broadcast_in_dim | solution.py:444
  2.0 66.1 %shard_map.77 = (bf16[256,1024]{1,0:T(8,128)(2,1)}, bf16[16,1024]{1,0:T(8,128)(2,1)}) custom-call(s32[4]{0:T(128)} %lengths.1, bf16[256,1024]{1,0:T(8,128)(2,1)} %hist.1, bf16[16,1024]{1,0:T(8,128)(2,1)} %cand.1, s32[16,128]{1,0:T(8,128)} %broadcast_in_dim.2.users, bf16[1,1024,4096]{2,1,0:T(8,128)(2,1)} %w_in_hbm.1, bf16[1,1024,1024]{2,1,0:T(8,128)(2,1)} %w_out_hbm.1), custom_call_target="tpu_custom_call" | custom-call | tf_op jit(solution)/shard_map/pallas_call | solution.py:449
  68.1 1.9 %copy.10 = bf16[256,1024]{1,0:T(8,128)(2,1)} copy(bf16[256,1024]{1,0:T(8,128)(2,1)} %get-tuple-element.4) | data formatting | bytes 1048576
  70.0 1.4 %copy.11 = bf16[16,1024]{1,0:T(8,128)(2,1)} copy(bf16[16,1024]{1,0:T(8,128)(2,1)} %get-tuple-element.5) | data formatting | bytes 65536

commit v2 on v1

--- a/solution.py
+++ b/solution.py
@@ -39,7 +39,7 @@
     lengths,
     hist,
     cand,
-    users,
+    users_row,
     w_in_hbm,
     w_out_hbm,
     out_ref,
@@ -59,6 +59,9 @@
     buf1,
     buf2,
     buf3,
+    out2,
+    out3,
+    users,
     w_sem,
     x_send,
     x_recv,
@@ -95,6 +98,10 @@
     for c in (2, 3, 1, 0, 4):
         w_copies[c].start()
 
+    eye = lax.broadcasted_iota(jnp.int32, (cr, cr), 0) == lax.broadcasted_iota(jnp.int32, (cr, cr), 1)
+    column = jnp.sum(jnp.where(eye, users_row[...], 0), axis=1, keepdims=True)
+    users[...] = jnp.broadcast_to(column, users.shape)
+
     barrier = pltpu.get_barrier_semaphore()
     pl.semaphore_signal(barrier, inc=1, device_id={"seq": sibling}, device_id_type=pl.DeviceIdType.MESH)
     pl.semaphore_signal(barrier, inc=1, device_id={"seq": partner}, device_id_type=pl.DeviceIdType.MESH)
@@ -151,13 +158,13 @@
         def _():
             x_copy(None, ROW + r, h, 0, up).start()
 
-        @pl.when(p == 0)
-        def _():
-            x_copy(None, own_slot, h, 1, partner).start()
-
         @pl.when(k == 0)
         def _():
             x_copy(None, own_slot, h, 2, sibling).start()
+
+    @pl.when(p == 0)
+    def _():
+        x_copy(None, own_slot, 0, 1, partner).start()
 
     ends = []
     total = jnp.int32(0)
@@ -209,6 +216,12 @@
     ]
     for c in to_partner:
         c.start()
+    for h in range(1, CHUNKS):
+
+        @pl.when(p == 0)
+        def _():
+            x_copy(None, own_slot, h, 1, partner).start()
+
     w_copies[1].wait()
     own_kv[1] = project(normed, 1)
     for c in to_partner:
@@ -229,11 +242,11 @@
         return remote(part.at[pl.ds(2 - 2 * k, 2)], buf1, cx_send.at[4], cx_recv.at[4], sibling)
 
     def red2():
-        return remote(part.at[k * 2 + 1 - p], buf2, cx_send.at[5], cx_recv.at[5], partner)
+        return remote(out2, buf2, cx_send.at[5], cx_recv.at[5], partner)
 
     def red3(d):
         to_row = (z + d) % depth
-        src = part.at[me_block, pl.ds(pl.multiple_of(to_row * cr, cr), cr)]
+        src = out3.at[pl.ds(pl.multiple_of(to_row * cr, cr), cr)]
         return remote(src, buf3.at[d], rz_send.at[d], rz_recv.at[d], (s + ROW * d) % n)
 
     block_rows = depth * cr
@@ -269,24 +282,33 @@
     def needed(slot, of):
         return (slot > of) & (slot < 2 * ROW + of) & (z - 2 + slot // ROW >= 0)
 
-    def pair(j, carry):
+    def pair_of(j):
         base = 2 * ROW - ROW * (j // 2)
-        swap = jnp.minimum(j // 2, 1) * p
-        first = base + 2 * ((j + swap) % 2)
-        mine = first + k
-
-        def hop(h, go_up, go_across):
-            pieces = pl.ds(h * piece, piece)
+        swap = min(j // 2, 1) * p if isinstance(j, int) else jnp.minimum(j // 2, 1) * p
+        return base + 2 * ((j + swap) % 2)
+
+    def hop(j, h):
+        mine = pair_of(j) + k
+        pieces = pl.ds(h * piece, piece)
+        came = [p == 1, None, z >= 1, z >= 1, (z >= 2) & (k == 1), (z >= 2) & (p == 0)][j]
+
+        @pl.when(came)
+        def _():
             pltpu.make_async_copy(hist.at[pieces], wnd.at[mine, pieces], x_recv.at[mine, h]).wait()
-            if go_up:
-
-                @pl.when((z + 1 < depth) & (r >= 1))
+            if j == 2:
+
+                @pl.when((z + 1 < depth) & (k == 1))
                 def _():
                     x_copy(mine, mine - ROW, h, 3, up).start()
 
-            if go_across == 1:
                 x_copy(mine, mine, h, 4, partner).start()
-            if go_across == 2:
+            if j == 3:
+
+                @pl.when((z + 1 < depth) & (r == 0))
+                def _():
+                    x_copy(mine, mine - ROW, h, 11, up).start()
+
+            if j == 4:
 
                 @pl.when(p == 1)
                 def _():
@@ -294,73 +316,73 @@
 
             @pl.when(needed(mine, r + 1 - 2 * k))
             def _():
-                x_copy(mine, mine, h, 6 + j, sibling).start()
-
-        @pl.when((j == 0) & (p == 1))
-        def _():
-            for h in range(CHUNKS):
-                hop(h, False, 0)
-
-        @pl.when((j == 2) & (z >= 1))
-        def _():
-            for h in range(CHUNKS):
-                hop(h, True, 1)
-
-        @pl.when((j == 3) & (z >= 1))
-        def _():
-            for h in range(CHUNKS):
-                hop(h, False, 0)
-
-        @pl.when((j == 4) & (z >= 2) & (r >= 1))
-        def _():
-            for h in range(CHUNKS):
-                hop(h, False, 2)
-
-        @pl.when((j == 5) & (z >= 2) & (p == 0))
-        def _():
-            for h in range(CHUNKS):
-                hop(h, False, 0)
-
-        @pl.when(j == 2)
-        def _():
-            red1().wait_recv()
-            part[pl.ds(2 * k, 2)] += buf1[...]
-            red2().start()
-
-        @pl.when(j == 3)
-        def _():
-            red2().wait_recv()
-            part[me_block] += buf2[...]
-
-            def send(d, c):
-                red3(d).start()
-                return c
-
-            lax.fori_loop(1, depth, send, 0)
-
-        def one(m, c):
-            slot = first + (k + m) % 2
-
-            @pl.when(needed(slot, r))
+                x_copy(mine, mine, h, (6, None, 7, 8, 9, 10)[j], sibling).start()
+
+    def all_hops(j, first):
+        for h in range(first, CHUNKS):
+            hop(j, h)
+
+    def sums_across():
+        red1().wait_recv()
+        part[pl.ds(2 * k, 2)] += buf1[...]
+        out2[...] = part[k * 2 + 1 - p].astype(bf16)
+        red2().start()
+
+    def sums_up():
+        red2().wait_recv()
+        part[me_block] += buf2[...].astype(f32)
+        out3[...] = part[me_block].astype(bf16)
+
+        def send(d, c):
+            red3(d).start()
+            return c
+
+        lax.fori_loop(1, depth, send, 0)
+
+    def event(e):
+        if e == 0:
+            hop(2, 0)
+            sums_across()
+            all_hops(2, 1)
+            all_hops(0, 0)
+        if e == 2:
+            hop(3, 0)
+        if e == 4:
+            all_hops(3, 1)
+            sums_up()
+        if e == 6:
+            all_hops(4, 0)
+        if e == 8:
+            all_hops(5, 0)
+
+    def one(e, carry):
+        for at in (0, 2, 4, 6, 8):
+
+            @pl.when(e == at)
             def _():
-                @pl.when(m == 1)
-                def _():
-                    for h in range(CHUNKS):
-                        pieces = pl.ds(h * piece, piece)
-                        pltpu.make_async_copy(
-                            hist.at[pieces], wnd.at[slot, pieces], x_recv.at[slot, h]
-                        ).wait()
-
-                norm = layer_norm(wnd[slot].astype(f32)).astype(bf16)
-                kv_s[0] = project(norm, 3)
-                kv_s[1] = project(norm, 1)
-                attend(kv_s, (z - 2) * ROW + slot)
-
-            return c
-
-        return lax.fori_loop(0, 2, one, carry)
-
-    lax.fori_loop(0, 6, pair, 0)
+                event(at)
+
+        m = e % 2
+        slot = pair_of(e // 2) + (k + m) % 2
+
+        @pl.when(needed(slot, r))
+        def _():
+            @pl.when(m == 1)
+            def _():
+                for h in range(CHUNKS):
+                    pieces = pl.ds(h * piece, piece)
+                    pltpu.make_async_copy(
+                        hist.at[pieces], wnd.at[slot, pieces], x_recv.at[slot, h]
+                    ).wait()
+
+            norm = layer_norm(wnd[slot].astype(f32)).astype(bf16)
+            kv_s[0] = project(norm, 3)
+            kv_s[1] = project(norm, 1)
+            attend(kv_s, (z - 2) * ROW + slot)
+
+        return carry
+
+    lax.fori_loop(0, 12, one, 0)
 
     w_copies[4].wait()
     y = (layer_norm(acc[...]) * u_s[...].astype(f32)).astype(bf16)
@@ -370,7 +392,7 @@
 
     def take(d, c):
         red3(d).wait_recv()
-        return c + buf3[d]
+        return c + buf3[d].astype(f32)
 
     mine_sum = part[me_block, mine_at]
     cattn = lax.fori_loop(1, depth, take, mine_sum)
@@ -401,7 +423,7 @@
         def _():
             x_copy(None, own_slot, h, 2, sibling).wait_send()
 
-        @pl.when((z >= 1) & (z + 1 < depth) & (r >= 1))
+        @pl.when((z >= 1) & (z + 1 < depth) & (k == 1))
         def _():
             x_copy(ROW + r, r, h, 3, up).wait_send()
 
@@ -409,39 +431,35 @@
         def _():
             x_copy(ROW + r, ROW + r, h, 4, partner).wait_send()
 
-        @pl.when((z >= 2) & (p == 1))
+        @pl.when((z >= 2) & (r == 3))
         def _():
             x_copy(r, r, h, 5, partner).wait_send()
 
         other = r + 1 - 2 * k
         across = 2 * (1 - p) + k
 
-        @pl.when((p == 1) & needed(2 * ROW + k, other))
-        def _():
-            x_copy(2 * ROW + k, 2 * ROW + k, h, 6, sibling).wait_send()
-
-        @pl.when((z >= 1) & needed(ROW + r, other))
-        def _():
-            x_copy(ROW + r, ROW + r, h, 8, sibling).wait_send()
-
-        @pl.when((z >= 1) & needed(ROW + across, other))
-        def _():
-            x_copy(ROW + across, ROW + across, h, 9, sibling).wait_send()
-
-        @pl.when((z >= 2) & (r >= 1) & needed(r, other))
-        def _():
-            x_copy(r, r, h, 10, sibling).wait_send()
-
-        @pl.when((z >= 2) & (p == 0) & needed(across, other))
-        def _():
-            x_copy(across, across, h, 11, sibling).wait_send()
+        @pl.when((z >= 1) & (z + 1 < depth) & (r == 0))
+        def _():
+            x_copy(ROW + across, across, h, 11, up).wait_send()
+
+        for kind, came, slot in (
+            (6, p == 1, 2 * ROW + k),
+            (7, z >= 1, ROW + r),
+            (8, z >= 1, ROW + across),
+            (9, (z >= 2) & (k == 1), r),
+            (10, (z >= 2) & (p == 0), across),
+        ):
+
+            @pl.when(came & needed(slot, other))
+            def _():
+                x_copy(slot, slot, h, kind, sibling).wait_send()
 
 
 def per_device(n, history, candidates, lengths, cand_user, w_in, w_out):
     rows, width = history.shape
     cr = candidates.shape[0]
     depth = n // ROW
-    users = jnp.broadcast_to(cand_user[:, None], (cr, 128))
+    users = cand_user[None, :]
     vmem = pl.BlockSpec(memory_space=pltpu.VMEM)
     dma = pltpu.SemaphoreType.DMA
     block = depth * cr
@@ -475,8 +493,11 @@
             pltpu.VMEM((many, width), bf16),
             pltpu.VMEM((ROW, block, width), f32),
             pltpu.VMEM((2, block, width), f32),
-            pltpu.VMEM((block, width), f32),
-            pltpu.VMEM((depth, cr, width), f32),
+            pltpu.VMEM((block, width), bf16),
+            pltpu.VMEM((depth, cr, width), bf16),
+            pltpu.VMEM((block, width), bf16),
+            pltpu.VMEM((block, width), bf16),
+            pltpu.VMEM((cr, 128), jnp.int32),
             dma((5,)),
             dma((12, CHUNKS)),
             dma((3 * ROW, CHUNKS)),

time: 71.6 us -> 59.7 us (0.83)
  the two profiles are of different devices: /device:TPU:17 before, /device:TPU:28 now
where the time goes in v2:
time: 59.7 us; the launch traced here: 59.5 us
  Pallas kernels  55.6 us (93%)
  local copies, waits for them, and re-layouts  3.24 us (5%)
  between operations  0.64 us (1%)
    pallas_call x1, Pallas kernels, per_device(): pl.pallas_call(functools.partial(kernel, n), out_shape=(jax.ShapeDtypeStr...  55.6 us
    unnamed x2, local copies, waits for them, and re-layouts  3.24 us

profile of v2, /device:TPU:28, one launch (start us, length us, event | category | flops | bytes accessed | tf_op | source)
XLA Modules:
  0.0 59.5 jit_solution(12555594687710600408)
XLA Ops:
  0.6 55.6 %shard_map.77 = (bf16[256,1024]{1,0:T(8,128)(2,1)}, bf16[16,1024]{1,0:T(8,128)(2,1)}) custom-call(s32[4]{0:T(128)} %lengths.1, bf16[256,1024]{1,0:T(8,128)(2,1)} %hist.1, bf16[16,1024]{1,0:T(8,128)(2,1)} %cand.1, s32[1,16]{1,0:T(1,128)} %bitcast.1, bf16[1,1024,4096]{2,1,0:T(8,128)(2,1)} %w_in_hbm.1, bf16[1,1024,1024]{2,1,0:T(8,128)(2,1)} %w_out_hbm.1), custom_call_target="tpu_custom_call" | custom-call | tf_op jit(solution)/shard_map/pallas_call | solution.py:467
  56.2 1.9 %copy.10 = bf16[256,1024]{1,0:T(8,128)(2,1)} copy(bf16[256,1024]{1,0:T(8,128)(2,1)} %get-tuple-element.4) | data formatting | bytes 1048576
  58.1 1.4 %copy.11 = bf16[16,1024]{1,0:T(8,128)(2,1)} copy(bf16[16,1024]{1,0:T(8,128)(2,1)} %get-tuple-element.5) | data formatting | bytes 65536

commit v3 on v2

--- a/solution.py
+++ b/solution.py
@@ -9,7 +9,7 @@
 
 HEADS = 8
 WIN = 8
-CHUNKS = 2
+CHUNKS = 4
 ROW = 4
 
 eps = 1e-06
@@ -62,6 +62,7 @@
     out2,
     out3,
     users,
+    uc_s,
     w_sem,
     x_send,
     x_recv,
@@ -116,6 +117,9 @@
         return carry
 
     lax.fori_loop(1, depth, greet, 0)
+    own_slot = 2 * ROW + r
+    normed = layer_norm(hist[...].astype(f32)).astype(bf16)
+    wnd[own_slot] = normed
     pl.semaphore_wait(barrier, depth + 1)
 
     def remote(src, dst, send, recv, to):
@@ -130,10 +134,8 @@
 
     def x_copy(src_slot, dst_slot, h, kind, to):
         part_rows = pl.ds(h * piece, piece)
-        src = hist.at[part_rows] if src_slot is None else wnd.at[src_slot, part_rows]
-        return remote(src, wnd.at[dst_slot, part_rows], x_send.at[kind, h], x_recv.at[dst_slot, h], to)
-
-    own_slot = 2 * ROW + r
+        return remote(wnd.at[src_slot, part_rows], wnd.at[dst_slot, part_rows], x_send.at[kind, h], x_recv.at[dst_slot, h], to)
+
     up = (s + ROW) % n
 
     me_block = k * 2 + p
@@ -156,15 +158,17 @@
 
         @pl.when(z + 1 < depth)
         def _():
-            x_copy(None, ROW + r, h, 0, up).start()
+            x_copy(own_slot, ROW + r, h, 0, up).start()
+
+        if h == 0:
+
+            @pl.when(p == 0)
+            def _():
+                x_copy(own_slot, own_slot, h, 1, partner).start()
 
         @pl.when(k == 0)
         def _():
-            x_copy(None, own_slot, h, 2, sibling).start()
-
-    @pl.when(p == 0)
-    def _():
-        x_copy(None, own_slot, 0, 1, partner).start()
+            x_copy(own_slot, own_slot, h, 2, sibling).start()
 
     ends = []
     total = jnp.int32(0)
@@ -193,16 +197,59 @@
             weight = jnp.where(ok, silu_of_twice(half), 0.0).astype(bf16)
             acc[:, cols] += dot(weight, kv[1, :, cols])
 
+    def needed(slot, of):
+        return (slot > of) & (slot < 2 * ROW + of) & (z - 2 + slot // ROW >= 0)
+
+    def pair_of(j):
+        base = 2 * ROW - ROW * (j // 2)
+        swap = min(j // 2, 1) * p if isinstance(j, int) else jnp.minimum(j // 2, 1) * p
+        return base + 2 * ((j + swap) % 2)
+
+    def hop(j, h):
+        mine = pair_of(j) + k
+        pieces = pl.ds(h * piece, piece)
+        came = [p == 1, None, z >= 1, z >= 1, (z >= 2) & (k == 1), (z >= 2) & (p == 0)][j]
+
+        @pl.when(came)
+        def _():
+            pltpu.make_async_copy(hist.at[pieces], wnd.at[mine, pieces], x_recv.at[mine, h]).wait()
+            if j == 2:
+
+                @pl.when((z + 1 < depth) & (k == 1))
+                def _():
+                    x_copy(mine, mine - ROW, h, 3, up).start()
+
+                x_copy(mine, mine, h, 4, partner).start()
+            if j == 3:
+
+                @pl.when((z + 1 < depth) & (r == 0))
+                def _():
+                    x_copy(mine, mine - ROW, h, 11, up).start()
+
+            if j == 4:
+
+                @pl.when(p == 1)
+                def _():
+                    x_copy(mine, mine, h, 5, partner).start()
+
+            @pl.when(needed(mine, r + 1 - 2 * k))
+            def _():
+                x_copy(mine, mine, h, (6, None, 7, 8, 9, 10)[j], sibling).start()
+
+    def all_hops(j, first):
+        for h in range(first, CHUNKS):
+            hop(j, h)
+
     acc[...] = jnp.zeros_like(acc)
-    normed = layer_norm(hist[...].astype(f32)).astype(bf16)
+    mine_at = pl.ds(pl.multiple_of(z * cr, cr), cr)
+    cbuf[me_block, mine_at] = cand[...]
+    ubuf[me_block, mine_at] = users[...]
     w_copies[2].wait()
     q_s[...] = project(normed, 2)
     w_copies[3].wait()
     own_kv[0] = project(normed, 3)
-
-    mine_at = pl.ds(pl.multiple_of(z * cr, cr), cr)
-    cbuf[me_block, mine_at] = cand[...]
-    ubuf[me_block, mine_at] = users[...]
+    w_copies[1].wait()
+    own_kv[1] = project(normed, 1)
 
     def cz_wait(d, carry):
         cz_copy(d, 0).wait_recv()
@@ -220,10 +267,13 @@
 
         @pl.when(p == 0)
         def _():
-            x_copy(None, own_slot, h, 1, partner).start()
-
-    w_copies[1].wait()
-    own_kv[1] = project(normed, 1)
+            x_copy(own_slot, own_slot, h, 1, partner).start()
+
+    hop(2, 0)
+    w_copies[0].wait()
+    u_s[...] = project(normed, 0)
+    attend(own_kv, s)
+    hop(2, 1)
     for c in to_partner:
         c.wait_recv()
     to_sibling = [
@@ -232,9 +282,9 @@
     ]
     for c in to_sibling:
         c.start()
-    w_copies[0].wait()
-    u_s[...] = project(normed, 0)
-    attend(own_kv, s)
+    u_c = project(layer_norm(cand[...].astype(f32)).astype(bf16), 0)
+    uc_s[...] = u_c
+    hop(2, 2)
     for c in to_sibling:
         c.wait_recv()
 
@@ -279,49 +329,6 @@
         lax.fori_loop(0, ROW // count, cand_block, 0)
     red1().start()
 
-    def needed(slot, of):
-        return (slot > of) & (slot < 2 * ROW + of) & (z - 2 + slot // ROW >= 0)
-
-    def pair_of(j):
-        base = 2 * ROW - ROW * (j // 2)
-        swap = min(j // 2, 1) * p if isinstance(j, int) else jnp.minimum(j // 2, 1) * p
-        return base + 2 * ((j + swap) % 2)
-
-    def hop(j, h):
-        mine = pair_of(j) + k
-        pieces = pl.ds(h * piece, piece)
-        came = [p == 1, None, z >= 1, z >= 1, (z >= 2) & (k == 1), (z >= 2) & (p == 0)][j]
-
-        @pl.when(came)
-        def _():
-            pltpu.make_async_copy(hist.at[pieces], wnd.at[mine, pieces], x_recv.at[mine, h]).wait()
-            if j == 2:
-
-                @pl.when((z + 1 < depth) & (k == 1))
-                def _():
-                    x_copy(mine, mine - ROW, h, 3, up).start()
-
-                x_copy(mine, mine, h, 4, partner).start()
-            if j == 3:
-
-                @pl.when((z + 1 < depth) & (r == 0))
-                def _():
-                    x_copy(mine, mine - ROW, h, 11, up).start()
-
-            if j == 4:
-
-                @pl.when(p == 1)
-                def _():
-                    x_copy(mine, mine, h, 5, partner).start()
-
-            @pl.when(needed(mine, r + 1 - 2 * k))
-            def _():
-                x_copy(mine, mine, h, (6, None, 7, 8, 9, 10)[j], sibling).start()
-
-    def all_hops(j, first):
-        for h in range(first, CHUNKS):
-            hop(j, h)
-
     def sums_across():
         red1().wait_recv()
         part[pl.ds(2 * k, 2)] += buf1[...]
@@ -341,29 +348,27 @@
 
     def event(e):
         if e == 0:
-            hop(2, 0)
+            hop(2, 3)
             sums_across()
-            all_hops(2, 1)
+        if e == 2:
             all_hops(0, 0)
-        if e == 2:
-            hop(3, 0)
-        if e == 4:
-            all_hops(3, 1)
+        if e == 5:
             sums_up()
-        if e == 6:
-            all_hops(4, 0)
-        if e == 8:
-            all_hops(5, 0)
+        for j, h in {2: ((3, 0),), 3: ((3, 1),), 4: ((3, 2), (4, 0)), 5: ((3, 3), (4, 1)), 6: ((4, 2),), 7: ((4, 3),), 8: ((5, 0), (5, 1)), 9: ((5, 2),), 10: ((5, 3),)}.get(e, ()):
+            hop(j, h)
 
     def one(e, carry):
-        for at in (0, 2, 4, 6, 8):
+        for at in (0, 2, 3, 4, 5, 6, 7, 8, 9, 10):
 
             @pl.when(e == at)
             def _():
                 event(at)
 
+        step = e // 2
+        late = jnp.minimum(step // 3, 1)
+        j = (1 - late) * ((step + 2) % 3) + late * step
         m = e % 2
-        slot = pair_of(e // 2) + (k + m) % 2
+        slot = pair_of(j) + (k + m) % 2
 
         @pl.when(needed(slot, r))
         def _():
@@ -375,7 +380,7 @@
                         hist.at[pieces], wnd.at[slot, pieces], x_recv.at[slot, h]
                     ).wait()
 
-            norm = layer_norm(wnd[slot].astype(f32)).astype(bf16)
+            norm = wnd[slot]
             kv_s[0] = project(norm, 3)
             kv_s[1] = project(norm, 1)
             attend(kv_s, (z - 2) * ROW + slot)
@@ -385,19 +390,17 @@
     lax.fori_loop(0, 12, one, 0)
 
     w_copies[4].wait()
-    y = (layer_norm(acc[...]) * u_s[...].astype(f32)).astype(bf16)
-    out_ref[...] = (hist[...].astype(f32) + dot(y, w_out[...])).astype(bf16)
-
-    u_c = project(layer_norm(cand[...].astype(f32)).astype(bf16), 0)
 
     def take(d, c):
         red3(d).wait_recv()
         return c + buf3[d].astype(f32)
 
-    mine_sum = part[me_block, mine_at]
-    cattn = lax.fori_loop(1, depth, take, mine_sum)
-    y_c = (layer_norm(cattn) * u_c.astype(f32)).astype(bf16)
-    cout_ref[...] = (cand[...].astype(f32) + dot(y_c, w_out[...])).astype(bf16)
+    cattn = lax.fori_loop(1, depth, take, part[me_block, mine_at])
+    y_c = (layer_norm(cattn) * uc_s[...].astype(f32)).astype(bf16)
+    y = (layer_norm(acc[...]) * u_s[...].astype(f32)).astype(bf16)
+    both = dot(jnp.concatenate([y, y_c], axis=0), w_out[...])
+    out_ref[...] = (hist[...].astype(f32) + both[:rows]).astype(bf16)
+    cout_ref[...] = (cand[...].astype(f32) + both[rows:]).astype(bf16)
 
     for c in to_partner + to_sibling + [red1(), red2()]:
         c.wait_send()
@@ -413,15 +416,15 @@
 
         @pl.when(z + 1 < depth)
         def _():
-            x_copy(None, ROW + r, h, 0, up).wait_send()
+            x_copy(own_slot, ROW + r, h, 0, up).wait_send()
 
         @pl.when(p == 0)
         def _():
-            x_copy(None, own_slot, h, 1, partner).wait_send()
+            x_copy(own_slot, own_slot, h, 1, partner).wait_send()
 
         @pl.when(k == 0)
         def _():
-            x_copy(None, own_slot, h, 2, sibling).wait_send()
+            x_copy(own_slot, own_slot, h, 2, sibling).wait_send()
 
         @pl.when((z >= 1) & (z + 1 < depth) & (k == 1))
         def _():
@@ -498,6 +501,7 @@
             pltpu.VMEM((block, width), bf16),
             pltpu.VMEM((block, width), bf16),
             pltpu.VMEM((cr, 128), jnp.int32),
+            pltpu.VMEM((cr, width), bf16),
             dma((5,)),
             dma((12, CHUNKS)),
             dma((3 * ROW, CHUNKS)),

time: 59.7 us -> 51.4 us (0.86)
  the two profiles are of different devices: /device:TPU:28 before, /device:TPU:17 now
where the time goes in v3:
time: 51.4 us; the launch traced here: 51.1 us
  Pallas kernels  47.2 us (92%)
  local copies, waits for them, and re-layouts  3.24 us (6%)
  between operations  0.64 us (1%)
    pallas_call x1, Pallas kernels, per_device(): pl.pallas_call(functools.partial(kernel, n), out_shape=(jax.ShapeDtypeStr...  47.2 us
    unnamed x2, local copies, waits for them, and re-layouts  3.24 us

profile of v3, /device:TPU:17, one launch (start us, length us, event | category | flops | bytes accessed | tf_op | source)
XLA Modules:
  0.0 51.1 jit_solution(7961501162576313668)
XLA Ops:
  0.6 47.2 %shard_map.77 = (bf16[256,1024]{1,0:T(8,128)(2,1)}, bf16[16,1024]{1,0:T(8,128)(2,1)}) custom-call(s32[4]{0:T(128)} %lengths.1, bf16[256,1024]{1,0:T(8,128)(2,1)} %hist.1, bf16[16,1024]{1,0:T(8,128)(2,1)} %cand.1, s32[1,16]{1,0:T(1,128)} %bitcast.1, bf16[1,1024,4096]{2,1,0:T(8,128)(2,1)} %w_in_hbm.1, bf16[1,1024,1024]{2,1,0:T(8,128)(2,1)} %w_out_hbm.1), custom_call_target="tpu_custom_call" | custom-call | tf_op jit(solution)/shard_map/pallas_call | solution.py:470
  47.9 1.9 %copy.10 = bf16[256,1024]{1,0:T(8,128)(2,1)} copy(bf16[256,1024]{1,0:T(8,128)(2,1)} %get-tuple-element.4) | data formatting | bytes 1048576
  49.7 1.4 %copy.11 = bf16[16,1024]{1,0:T(8,128)(2,1)} copy(bf16[16,1024]{1,0:T(8,128)(2,1)} %get-tuple-element.5) | data formatting | bytes 65536

commit v4 on v3

--- a/solution.py
+++ b/solution.py
@@ -349,16 +349,17 @@
     def event(e):
         if e == 0:
             hop(2, 3)
+        if e == 1:
             sums_across()
         if e == 2:
             all_hops(0, 0)
-        if e == 5:
+        if e == 7:
             sums_up()
-        for j, h in {2: ((3, 0),), 3: ((3, 1),), 4: ((3, 2), (4, 0)), 5: ((3, 3), (4, 1)), 6: ((4, 2),), 7: ((4, 3),), 8: ((5, 0), (5, 1)), 9: ((5, 2),), 10: ((5, 3),)}.get(e, ()):
+        for j, h in {2: ((3, 0),), 3: ((3, 1), (4, 0)), 4: ((3, 2), (4, 1)), 5: ((3, 3), (4, 2)), 6: ((4, 3),), 7: ((5, 0),), 8: ((5, 1),), 9: ((5, 2),), 10: ((5, 3),)}.get(e, ()):
             hop(j, h)
 
     def one(e, carry):
-        for at in (0, 2, 3, 4, 5, 6, 7, 8, 9, 10):
+        for at in (0, 1, 2, 3, 4, 5, 6, 7, 8, 9, 10):
 
             @pl.when(e == at)
             def _():

time: 51.4 us -> 47.8 us (0.930)
  Pallas kernels: 47.2 us -> 43.3 us
    pallas_call x1, Pallas kernels: 47.2 us -> 43.3 us  [per_device(): pl.pallas_call(functools.partial(kernel, n), out_shape=(jax.ShapeDtypeStr...]
where the time goes in v4:
time: 47.8 us; the launch traced here: 47.2 us
  Pallas kernels  43.3 us (91%)
  local copies, waits for them, and re-layouts  3.24 us (7%)
  between operations  0.64 us (1%)
    pallas_call x1, Pallas kernels, per_device(): pl.pallas_call(functools.partial(kernel, n), out_shape=(jax.ShapeDtypeStr...  43.3 us
    unnamed x2, local copies, waits for them, and re-layouts  3.24 us

profile of v4, /device:TPU:17, one launch (start us, length us, event | category | flops | bytes accessed | tf_op | source)
XLA Modules:
  0.0 47.2 jit_solution(16268611951426830219)
XLA Ops:
  0.6 43.3 %shard_map.77 = (bf16[256,1024]{1,0:T(8,128)(2,1)}, bf16[16,1024]{1,0:T(8,128)(2,1)}) custom-call(s32[4]{0:T(128)} %lengths.1, bf16[256,1024]{1,0:T(8,128)(2,1)} %hist.1, bf16[16,1024]{1,0:T(8,128)(2,1)} %cand.1, s32[1,16]{1,0:T(1,128)} %bitcast.1, bf16[1,1024,4096]{2,1,0:T(8,128)(2,1)} %w_in_hbm.1, bf16[1,1024,1024]{2,1,0:T(8,128)(2,1)} %w_out_hbm.1), custom_call_target="tpu_custom_call" | custom-call | tf_op jit(solution)/shard_map/pallas_call | solution.py:471
  43.9 1.9 %copy.10 = bf16[256,1024]{1,0:T(8,128)(2,1)} copy(bf16[256,1024]{1,0:T(8,128)(2,1)} %get-tuple-element.4) | data formatting | bytes 1048576
  45.8 1.4 %copy.11 = bf16[16,1024]{1,0:T(8,128)(2,1)} copy(bf16[16,1024]{1,0:T(8,128)(2,1)} %get-tuple-element.5) | data formatting | bytes 65536
